TPU v7x, 32 devices: a whole 2x2x4 slice. The times are simulated.
32 devices in a mesh: parts: 2 (over y), tok: 4 (over z), hid: 4 (over x, core).
Axes of the slice: x: 2, y: 2, z: 4, core: 2. Of those that a mesh axis runs over, the one named last changes fastest.
Arguments:
- tokens: bfloat16 [6144, 8192], P(('parts', 'tok'), 'hid'), parts along dimension 0, may hold values from -6 to 6
- adapter_ids: int32 [6144, 1], P(('parts', 'tok')), parts along dimension 0, may hold values from 0 to 31; in each aligned block of 768 rows (0 to 767, 768 to 1535, ...) at most 72 rows name the same one
- value_weight: bfloat16 [8192, 1024], P('hid'), may hold values from -0.0625 to 0.0625
- adapter_down: bfloat16 [32, 16, 8192], P('tok', None, 'hid'), may hold values from -0.0625 to 0.0625
- adapter_up: bfloat16 [32, 16, 1024], P('tok', None, 'hid'), may hold values from -1.5 to 1.5
Outputs:
- value_out: bfloat16 [6144, 1024], P(('parts', 'tok'), 'hid'), parts along dimension 0
There are 2 independent parts, one for each index of `parts`. A program takes and returns all parts, laid end to end along the dimension named above; an argument that names none is the same for every part. Nothing has to cross between parts.
Inputs may be any that keep to these rules, and one draw needn't show every extreme that they name: `adapter_ids`: among the 768 tokens of one index of tok, each adapter id appears at most 72 times; in some of these aligned blocks one id appears exactly 72 times.
All inputs are finite; a program needn't handle non-finite values.
Results may differ from a plain program's by a relative error of at most 0.0048.
Values may be sent and summed in bfloat16 or wider, within the bound.
A program may use at most 128 MiB of HBM per device.

v0:
```python
import jax
import jax.numpy as jnp
from jax import lax
from jax.sharding import PartitionSpec as P


def per_device(tokens, adapter_ids, value_weight, adapter_down, adapter_up):
    tok_rows, d_local = tokens.shape
    n_tok = lax.axis_size("tok")
    adp_dev = adapter_down.shape[0]
    low_rank = adapter_down.shape[1]
    kv_local = adapter_up.shape[2]
    adapters_all = adp_dev * n_tok
    capacity = max(2, 3 * tok_rows // adapters_all)
    token_ids = adapter_ids[:, 0]
    matches = token_ids[:, None] == token_ids[None, :]
    before = lax.broadcasted_iota(jnp.int32, (tok_rows, tok_rows), 0) > lax.broadcasted_iota(
        jnp.int32, (tok_rows, tok_rows), 1
    )
    position = jnp.sum((matches & before).astype(jnp.int32), axis=1)
    slot_index = token_ids * capacity + position
    slot_rows = (
        jnp.zeros((adapters_all * capacity, d_local), jnp.bfloat16).at[slot_index].set(tokens)
    )
    base_sums = lax.psum_scatter(
        lax.dot_general(
            value_weight, tokens, (((0,), (1,)), ((), ())), preferred_element_type=jnp.float32
        ),
        "hid",
        scatter_dimension=0,
        tiled=True,
    )
    weights_piece = lax.all_gather(adapter_down, "tok", axis=0, tiled=True)
    piece_count = weights_piece.shape[0]
    slot_block = slot_rows
    slot_block = slot_block.reshape(piece_count, capacity, d_local)
    partial_piece = jnp.einsum(
        "acn,arn->rac", slot_block, weights_piece, preferred_element_type=jnp.float32
    )
    partial_piece = partial_piece.reshape(low_rank, piece_count * capacity)
    low_rows = lax.psum(partial_piece, "hid").astype(jnp.bfloat16)
    weights_piece = lax.all_gather(adapter_up, "tok", axis=0, tiled=True)
    piece_count = weights_piece.shape[0]
    low_block = low_rows
    low_block = low_block.reshape(low_rank, piece_count, capacity)
    expanded = jnp.einsum(
        "rac,ark->ack", low_block, weights_piece, preferred_element_type=jnp.float32
    )
    delta_slots = expanded.astype(jnp.bfloat16).reshape(piece_count * capacity, kv_local)
    delta_rows = delta_slots[slot_index]
    return (base_sums.T + delta_rows.astype(jnp.float32)).astype(jnp.bfloat16)


def solution(mesh):
    in_specs = (
        P(("parts", "tok"), "hid"),
        P(("parts", "tok"), None),
        P("hid", None),
        P("tok", None, "hid"),
        P("tok", None, "hid"),
    )
    out_specs = P(("parts", "tok"), "hid")
    return jax.shard_map(
        per_device, mesh=mesh, in_specs=in_specs, out_specs=out_specs, check_vma=False
    )
```

profile of v0, /device:TPU:0, one launch (start us, length us, event | category | flops | bytes accessed | tf_op | source)
XLA Modules:
  0.0 95.5 jit_solution(1115968050295311452)
XLA Ops:
  7.4 0.0 all-gather.2.cloned.1.call-start
  7.4 0.7 all-gather.2.cloned.1.call-update
  8.1 0.0 reduce-scatter.2.cloned.1.call-start
  8.1 8.3 %fusion.6 = f32[1024,768]{1,0:T(8,128)} fusion(bf16[2048,1024]{1,0:T(8,128)(2,1)} %param.7, bf16[768,2048]{1,0:T(8,128)(2,1)} %param.5), kind=kOutput, calls=%fused_computation.15 | convolution fusion | flops 3221225472 | bytes 10485760 | tf_op jit(solution)/shard_map/dot_general | solution.py:26
  16.4 0.0 copy-start.1
  16.4 0.0 reduce-scatter.2.cloned.1.call-update
  16.5 0.7 copy-done.1
  17.1 0.4 convert_reduce_fusion
  17.5 0.0 copy-start
  17.5 13.4 %scatter_custom_fusion = bf16[2304,2048]{1,0:T(8,128)(2,1)} fusion(s32[768]{0:T(1024)S(1)} %fusion.5, bf16[768,2048]{1,0:T(8,128)(2,1)} %param.5, bf16[]{:T(256)} %constant.4.clone.1), kind=kCustom, calls=%fused_computation.2 | custom fusion | bytes 9437696 | tf_op jit(solution)/shard_map/scatter | solution.py:23
  30.9 0.0 copy-done
  30.9 18.3 %all_gather.7 = bf16[32,16,256]{2,1,0:T(8,128)(2,1)S(1)} all-gather(bf16[8,16,256]{2,1,0:T(8,128)(2,1)S(1)} %copy-done), channel_id=1, replica_groups=mesh['parts'=2,'tok'=4,'hid'=4] {'tok'}, dimensions={0}, use_global_device_ids=true | all-gather | bytes 327680 | tf_op jit(solution)/shard_map/all_gather | solution.py:42
  49.2 13.1 %all-gather.2.cloned.1.call-done = bf16[32,16,2048]{2,1,0:T(8,128)(2,1)} async-done(((bf16[8,16,2048]{2,1,0:T(8,128)(2,1)}), bf16[32,16,2048]{2,1,0:T(8,128)(2,1)}) %all-gather.2.cloned.1.call-update) | async-done | bytes 2097168 | tf_op jit(solution)/shard_map/all_gather | solution.py:33
  62.4 6.8 %convolution_bitcast_fusion = f32[16,32,72]{2,0,1:T(8,128)S(1)} fusion(bf16[32,72,2048]{2,1,0:T(8,128)(2,1)} %bitcast.13, bf16[32,16,2048]{2,1,0:T(8,128)(2,1)} %all-gather.2.cloned.1.call-done), kind=kOutput, calls=%fused_computation.8 | convolution fusion | flops 150994944 | bytes 11681792 | tf_op jit(solution)/shard_map/acn,arn->rac/dot_general | solution.py:37
  69.2 0.1 copy.16
  69.3 0.2 reshape.15
  69.5 12.8 %all-reduce.1 = bf16[16,2304]{1,0:T(8,128)(2,1)S(1)} all-reduce(f32[16,2304]{1,0:T(8,128)S(1)} %reshape.15), channel_id=1, replica_groups=mesh['parts'=2,'tok'=4,'hid'=4] {'hid'}, use_global_device_ids=true, to_apply=%region_3.0 | all-reduce | flops 36864 | bytes 221184 | tf_op jit(solution)/shard_map/psum | solution.py:41
  82.3 0.3 reshape.16
  82.6 0.5 convolution_convert_fusion
  83.1 2.7 %gather_fusion = bf16[768,256]{1,0:T(8,128)(2,1)S(1)} fusion(bf16[2304,256]{1,0:T(8,128)(2,1)S(1)} %bitcast.14, s32[1024]{0:T(1024)S(1)} %pad_clamp_fusion), kind=kCustom, calls=%fused_computation | custom fusion | bytes 789504 | tf_op jit(solution)/shard_map/gather | solution.py:50
  85.7 0.2 copy.18
  85.9 0.0 reduce-scatter.2.cloned.1.call-done
  85.9 1.2 %fusion.3 = bf16[768,256]{0,1:T(8,128)(2,1)S(1)} fusion(f32[256,768]{1,0:T(8,128)} %reduce-scatter.2.cloned.1.call-done, bf16[768,256]{0,1:T(8,128)(2,1)S(1)} %copy.18), kind=kLoop, calls=%fused_computation.10 | loop fusion | flops 589824 | bytes 1572864 | tf_op jit(solution)/shard_map/convert_element_type | solution.py:51
  87.1 0.9 copy.19
  (3 shorter events, 0.0 us)
Async XLA Ops:
  7.4 55.0 %all-gather.2.cloned.1.call-start = ((), (), s32[]{:S(2)}) async-start(), calls=%async_computation.2 | async-start | bytes 2621440 | tf_op jit(solution)/shard_map/all_gather | solution.py:33
  8.1 77.8 %reduce-scatter.2.cloned.1.call-start = ((), (), s32[]{:S(2)}) async-start(), calls=%async_computation.1 | async-start | bytes 3932160 | tf_op jit(solution)/shard_map/reduce_scatter | solution.py:25
  16.4 0.7 copy-start.1
  17.5 13.4 %copy-start = (bf16[8,16,256]{2,1,0:T(8,128)(2,1)S(1)}, bf16[8,16,256]{2,1,0:T(8,128)(2,1)}, u32[]{:S(2)}) copy-start(bf16[8,16,256]{2,1,0:T(8,128)(2,1)} %param.9) | copy-start | bytes 196612
Sparse Core Ops, SparseCore 0:
  9.7 52.5 all-gather.1
Sparse Core Ops, SparseCore 1:
  16.5 40.4 reduce-scatter.1
where the time goes:
time: 95.7 us; the launch traced here: 95.5 us
  blocking collectives  31.1 us (32%)
  local copies, waits for them, and re-layouts  18.4 us (19%)
  matrix products  15.6 us (16%)
  between operations  14.9 us (16%)
  waiting for transfers between devices  13.9 us (15%)
  other arithmetic  1.6 us (2%)
    all_gather x1, blocking collectives, per_device(): weights_piece = lax.all_gather(adapter_up, 'tok', axis=0, tiled=True)  18.3 us
    scatter x1, local copies, waits for them, and re-layouts, per_device(): jnp.zeros((adapters_all * capacity, d_local), jnp.bfloat16).at[slot_index]  13.4 us
    all_gather x1, waiting for transfers between devices, per_device(): weights_piece = lax.all_gather(adapter_down, 'tok', axis=0, tiled=True)  13.1 us
    psum x1, blocking collectives, per_device(): low_rows = lax.psum(partial_piece, 'hid').astype(jnp.bfloat16)  12.8 us
    dot_general x1, matrix products, per_device(): lax.dot_general(value_weight, tokens, (((0,), (1,)), ((), ())), preferred...  8.29 us
    dot_general x1, matrix products, per_device(): jnp.einsum('acn,arn->rac', slot_block, weights_piece, preferred_element_t...  6.83 us
    gather x2, local copies, waits for them, and re-layouts, per_device(): delta_rows = delta_slots[slot_index]  2.83 us
  transfers between devices with their start and end apart: 2, of which 1 were waited for; matrix products, arithmetic and copies ran while one was open for 34% of the time, Pallas kernels for 0%

commit v1 on v0

v1 whole, which is shorter than its diff:
```python
import functools

import jax
import jax.numpy as jnp
from jax import lax
from jax.experimental import pallas as pl
from jax.experimental.pallas import tpu as pltpu
from jax.sharding import PartitionSpec as P

MESH = pl.DeviceIdType.MESH
F32 = jnp.float32
BF16 = jnp.bfloat16


def kernel(
    n_tok,
    n_hid,
    pieces,
    rank,
    ids_ref,
    tokens_hbm,
    value_hbm,
    down_hbm,
    up_hbm,
    out_ref,
    tokens,
    value,
    adapters,
    core_send,
    core_recv,
    partial,
    chip_send,
    chip_recv,
    picked,
    wanted,
    low_send,
    low_recv,
    load_sem,
    right_sem,
    left_sem,
    line_sem,
    pair_send_sem,
    pair_recv_sem,
    core_send_sem,
    core_recv_sem,
    chip_send_sem,
    chip_recv_sem,
    low_send_sem,
    low_recv_sem,
):
    y = lax.axis_index("parts")
    z = lax.axis_index("tok")
    h = lax.axis_index("hid")
    chips = n_hid // 2
    core = lax.rem(h, 2)
    x = lax.div(h, 2)
    rows, depth = tokens.shape
    kv = out_ref.shape[1]
    lanes = adapters.shape[1]
    adp_dev = lanes // rank
    half = lanes // 2
    piece = half // pieces

    load_down = pltpu.make_async_copy(down_hbm, adapters.at[z, :, pl.ds(0, depth)], load_sem.at[0])
    load_up = pltpu.make_async_copy(up_hbm, adapters.at[z, :, pl.ds(depth, kv)], load_sem.at[1])
    load_tokens = pltpu.make_async_copy(tokens_hbm, tokens, load_sem.at[2])
    load_value = pltpu.make_async_copy(value_hbm, value, load_sem.at[3])
    load_down.start()
    load_up.start()
    load_tokens.start()
    load_value.start()

    barrier = pltpu.get_barrier_semaphore()
    pl.semaphore_signal(barrier, inc=1, device_id={"parts": 1 - y}, device_id_type=MESH)
    for d in range(1, n_hid):
        pl.semaphore_signal(
            barrier, inc=1, device_id={"hid": lax.rem(h + d, n_hid)}, device_id_type=MESH
        )

    @pl.when(z > 0)
    def _():
        pl.semaphore_signal(barrier, inc=1, device_id={"tok": z - 1}, device_id_type=MESH)

    @pl.when(z < n_tok - 1)
    def _():
        pl.semaphore_signal(barrier, inc=1, device_id={"tok": z + 1}, device_id_type=MESH)

    neighbours = (z > 0).astype(jnp.int32) + (z < n_tok - 1).astype(jnp.int32)
    pl.semaphore_wait(barrier, n_hid + neighbours)

    def chunk(block, side, c):
        start = pl.multiple_of(side * half + c * piece, piece)
        return adapters.at[block, pl.ds(start, piece)]

    def to_right(block, c):
        ref = chunk(block, y, c)
        return pltpu.make_async_remote_copy(
            src_ref=ref,
            dst_ref=ref,
            send_sem=right_sem.at[block, c],
            recv_sem=line_sem.at[block, c],
            device_id={"tok": z + 1},
            device_id_type=MESH,
        )

    def to_left(block, c):
        ref = chunk(block, y, c)
        return pltpu.make_async_remote_copy(
            src_ref=ref,
            dst_ref=ref,
            send_sem=left_sem.at[block, c],
            recv_sem=line_sem.at[block, c],
            device_id={"tok": z - 1},
            device_id_type=MESH,
        )

    def to_pair(block, side, c):
        ref = chunk(block, side, c)
        return pltpu.make_async_remote_copy(
            src_ref=ref,
            dst_ref=ref,
            send_sem=pair_send_sem.at[block, c],
            recv_sem=pair_recv_sem.at[block, c],
            device_id={"parts": 1 - y},
            device_id_type=MESH,
        )

    load_down.wait()
    load_up.wait()
    for c in range(pieces):
        @pl.when(z < n_tok - 1)
        def _():
            to_right(z, c).start()

        @pl.when(z > 0)
        def _():
            to_left(z, c).start()

    def forward(s):
        from_left = z - 1 - s
        from_right = z + 1 + s
        for c in range(pieces):
            @pl.when(from_left >= 0)
            def _():
                to_right(from_left, c).wait_recv()

                @pl.when(z < n_tok - 1)
                def _():
                    to_right(from_left, c).start()

                to_pair(from_left, y, c).start()

            @pl.when(from_right < n_tok)
            def _():
                to_left(from_right, c).wait_recv()

                @pl.when(z > 0)
                def _():
                    to_left(from_right, c).start()

                to_pair(from_right, y, c).start()

    load_tokens.wait()
    load_value.wait()

    def base_block(j):
        columns = pl.ds(pl.multiple_of(j * kv, kv), kv)
        return jnp.dot(tokens[...], value[:, columns], preferred_element_type=F32)

    def to_core(i):
        return pltpu.make_async_remote_copy(
            src_ref=core_send.at[i],
            dst_ref=core_recv.at[i],
            send_sem=core_send_sem.at[i],
            recv_sem=core_recv_sem.at[i],
            device_id={"hid": x * 2 + 1 - core},
            device_id_type=MESH,
        )

    def other_core(i, carry):
        core_send[i] = base_block(i * 2 + 1 - core).astype(BF16)
        to_core(i).start()
        return carry

    lax.fori_loop(0, chips, other_core, 0)

    def own_core(i, carry):
        partial[i] = base_block(i * 2 + core)
        return carry

    lax.fori_loop(0, chips, own_core, 0)

    forward(0)

    def to_chip(i, slot):
        return pltpu.make_async_remote_copy(
            src_ref=chip_send.at[i],
            dst_ref=chip_recv.at[slot],
            send_sem=chip_send_sem.at[i],
            recv_sem=chip_recv_sem.at[slot],
            device_id={"hid": i * 2 + core},
            device_id_type=MESH,
        )

    for d in range(1, chips):
        i = lax.rem(x + d, chips)
        to_core(i).wait_recv()
        chip_send[i] = (partial[i] + core_recv[i].astype(F32)).astype(BF16)
        to_chip(i, x).start()

    lane_adapter = lax.broadcasted_iota(jnp.int32, (rows, lanes), 1) // rank
    ids = jnp.transpose(jnp.broadcast_to(ids_ref[...], (lanes, rows)))
    wanted[...] = ids - lane_adapter

    def low_block(block):
        sums = lax.dot_general(
            tokens[...],
            adapters[block, :, 0:depth],
            (((1,), (1,)), ((), ())),
            preferred_element_type=F32,
        )
        return jnp.where(wanted[...] == block * adp_dev, sums, 0.0)

    picked[...] = low_block(z)

    def low_of(s):
        for sign in (-1, 1):
            block = z + sign * (1 + s)

            @pl.when((block >= 0) & (block < n_tok))
            def _():
                for c in range(pieces):
                    to_pair(block, 1 - y, c).wait_recv()
                picked[...] += low_block(block)

    def step(s, carry):
        forward(s + 1)
        low_of(s)
        return carry

    lax.fori_loop(0, n_tok - 2, step, 0)

    to_core(x).wait_recv()
    partial[x] += core_recv[x].astype(F32)
    for d in range(1, chips):
        i = lax.rem(x + d, chips)
        to_chip(i, i).wait_recv()
        partial[x] += chip_recv[i].astype(F32)

    low_of(n_tok - 2)

    fold = (
        lax.rem(lax.broadcasted_iota(jnp.int32, (rank, lanes), 1), rank)
        == lax.broadcasted_iota(jnp.int32, (rank, lanes), 0)
    ).astype(F32).astype(BF16)
    low_send[...] = lax.dot_general(
        fold,
        picked[...].astype(BF16),
        (((1,), (1,)), ((), ())),
        preferred_element_type=F32,
    ).astype(BF16)

    def to_hid(d, slot):
        return pltpu.make_async_remote_copy(
            src_ref=low_send,
            dst_ref=low_recv.at[slot],
            send_sem=low_send_sem.at[d],
            recv_sem=low_recv_sem.at[slot],
            device_id={"hid": lax.rem(h + d, n_hid)},
            device_id_type=MESH,
        )

    for d in range(1, n_hid):
        to_hid(d, h).start()
    low = low_send[...].astype(F32)
    for d in range(1, n_hid):
        slot = lax.rem(h + d, n_hid)
        to_hid(d, slot).wait_recv()
        low += low_recv[slot].astype(F32)
    low = low.astype(BF16)

    spread = lax.dot_general(low, fold, (((0,), (0,)), ((), ())), preferred_element_type=F32)
    group = 4 if n_tok % 4 == 0 else 1
    delta = None
    for g in range(0, n_tok, group):
        chosen = jnp.concatenate(
            [
                jnp.where(wanted[...] == b * adp_dev, spread, 0.0).astype(BF16)
                for b in range(g, g + group)
            ],
            axis=1,
        )
        weights = adapters[g : g + group, :, depth : depth + kv].reshape(group * lanes, kv)
        term = jnp.dot(chosen, weights, preferred_element_type=F32)
        delta = term if delta is None else delta + term
    out_ref[...] = (partial[x] + delta.astype(BF16).astype(F32)).astype(BF16)

    for d in range(1, n_hid):
        to_hid(d, h).wait_send()
    for i in range(chips):
        to_core(i).wait_send()
    for d in range(1, chips):
        to_chip(lax.rem(x + d, chips), x).wait_send()

    def drain(block, carry):
        for c in range(pieces):
            @pl.when((block <= z) & (z < n_tok - 1))
            def _():
                to_right(block, c).wait_send()

            @pl.when((block >= z) & (z > 0))
            def _():
                to_left(block, c).wait_send()

            @pl.when(block != z)
            def _():
                to_pair(block, y, c).wait_send()

        return carry

    lax.fori_loop(0, n_tok, drain, 0)


def per_device(n_tok, n_hid, tokens, adapter_ids, value_weight, adapter_down, adapter_up):
    rows, depth = tokens.shape
    adp_dev, rank, kv = adapter_up.shape
    lanes = adp_dev * rank
    chips = n_hid // 2
    pieces = 4 if n_tok <= 8 else 1
    vmem = pl.BlockSpec(memory_space=pltpu.VMEM)
    hbm = pl.BlockSpec(memory_space=pl.ANY)
    dma = pltpu.SemaphoreType.DMA
    return pl.pallas_call(
        functools.partial(kernel, n_tok, n_hid, pieces, rank),
        out_shape=jax.ShapeDtypeStruct((rows, kv), BF16),
        in_specs=[vmem, hbm, hbm, hbm, hbm],
        out_specs=vmem,
        scratch_shapes=[
            pltpu.VMEM((rows, depth), BF16),
            pltpu.VMEM(value_weight.shape, BF16),
            pltpu.VMEM((n_tok, lanes, depth + kv), BF16),
            pltpu.VMEM((chips, rows, kv), BF16),
            pltpu.VMEM((chips, rows, kv), BF16),
            pltpu.VMEM((chips, rows, kv), F32),
            pltpu.VMEM((chips, rows, kv), BF16),
            pltpu.VMEM((chips, rows, kv), BF16),
            pltpu.VMEM((rows, lanes), F32),
            pltpu.VMEM((rows, lanes), jnp.int32),
            pltpu.VMEM((rank, rows), BF16),
            pltpu.VMEM((n_hid, rank, rows), BF16),
            dma((4,)),
            dma((n_tok, pieces)),
            dma((n_tok, pieces)),
            dma((n_tok, pieces)),
            dma((n_tok, pieces)),
            dma((n_tok, pieces)),
            dma((chips,)),
            dma((chips,)),
            dma((chips,)),
            dma((chips,)),
            dma((n_hid,)),
            dma((n_hid,)),
        ],
        compiler_params=pltpu.CompilerParams(
            collective_id=0, has_side_effects=True, vmem_limit_bytes=60 * 1024 * 1024
        ),
    )(
        adapter_ids.reshape(1, rows),
        tokens,
        value_weight,
        adapter_down.reshape(lanes, depth),
        adapter_up.reshape(lanes, kv),
    )


def solution(mesh):
    in_specs = (
        P(("parts", "tok"), "hid"),
        P(("parts", "tok"), None),
        P("hid", None),
        P("tok", None, "hid"),
        P("tok", None, "hid"),
    )
    out_specs = P(("parts", "tok"), "hid")
    body = functools.partial(per_device, mesh.shape["tok"], mesh.shape["hid"])
    return jax.shard_map(body, mesh=mesh, in_specs=in_specs, out_specs=out_specs, check_vma=False)
```

time: 95.7 us -> 39.4 us (0.41)
  Pallas kernels: 0 us -> 37.5 us
  blocking collectives: 31.1 us -> 0 us
  local copies, waits for them, and re-layouts: 18.4 us -> 1.77 us
  matrix products: 15.6 us -> 0 us
  between operations: 14.9 us -> 0.01 us
  waiting for transfers between devices: 13.9 us -> 0 us
  other arithmetic: 1.6 us -> 0 us
    pallas_call x0 -> x1, Pallas kernels: none -> 37.5 us  [per_device(): pl.pallas_call(functools.partial(kernel, n_tok, n_hid, pieces, rank), out...]
    all_gather x1 -> x0, blocking collectives: 18.3 us -> none  [per_device(): weights_piece = lax.all_gather(adapter_up, 'tok', axis=0, tiled=True)]
    dot_general x3 -> x0, matrix products: 15.6 us -> none  [the longest x1 8.29 us: per_device(): lax.dot_general(value_weight, tokens, (((0,), (1,)), ((), ())), preferred...]
    scatter x1 -> x0, local copies, waits for them, and re-layouts: 13.4 us -> none  [per_device(): jnp.zeros((adapters_all * capacity, d_local), jnp.bfloat16).at[slot_index]]
    all_gather x1 -> x0, waiting for transfers between devices: 13.1 us -> none  [per_device(): weights_piece = lax.all_gather(adapter_down, 'tok', axis=0, tiled=True)]
    psum x1 -> x0, blocking collectives: 12.8 us -> none  [per_device(): low_rows = lax.psum(partial_piece, 'hid').astype(jnp.bfloat16)]
    gather x2 -> x0, local copies, waits for them, and re-layouts: 2.83 us -> none  [per_device(): delta_rows = delta_slots[slot_index]]
    convert_element_type x1 -> x0, other arithmetic: 1.2 us -> none  [per_device(): return (base_sums.T + delta_rows.astype(jnp.float32)).astype(jnp.bfloat16)]
  transfers between devices with their start and end apart: 2 -> 0, of which waited for: 1 -> 0; matrix products, arithmetic and copies ran while one was open for 34% -> 0% of each run, Pallas kernels for 0% -> 0%
where the time goes in v1:
time: 39.4 us; the launch traced here: 39.3 us
  Pallas kernels  37.5 us (95%)
  local copies, waits for them, and re-layouts  1.77 us (4%)
    pallas_call x1, Pallas kernels, per_device(): pl.pallas_call(functools.partial(kernel, n_tok, n_hid, pieces, rank), out...  37.5 us
    unnamed x1, local copies, waits for them, and re-layouts  1.77 us

profile of v1, /device:TPU:0, one launch (start us, length us, event | category | flops | bytes accessed | tf_op | source)
XLA Modules:
  0.0 39.3 jit_solution(12934585356225236330)
XLA Ops:
  0.0 37.5 %shard_map.55 = bf16[768,256]{1,0:T(8,128)(2,1)} custom-call(s32[1,768]{1,0:T(1,128)} %bitcast.5, bf16[768,2048]{1,0:T(8,128)(2,1)} %tokens_hbm.1, bf16[2048,1024]{1,0:T(8,128)(2,1)} %value_hbm.1, bf16[128,2048]{1,0:T(8,128)(2,1)} %bitcast.3, bf16[128,256]{1,0:T(8,128)(2,1)} %bitcast.4), custom_call_target="tpu_custom_call" | custom-call | tf_op jit(solution)/shard_map/pallas_call | solution.py:333
  37.5 1.8 %copy.7 = bf16[768,256]{1,0:T(8,128)(2,1)} copy(bf16[768,256]{1,0:T(8,128)(2,1)} %shard_map.55) | data formatting | bytes 786432

commit v2 on v1

--- a/solution.py
+++ b/solution.py
@@ -136,10 +136,10 @@
         def _():
             to_left(z, c).start()
 
-    def forward(s):
+    def forward(s, first, last):
         from_left = z - 1 - s
         from_right = z + 1 + s
-        for c in range(pieces):
+        for c in range(first, last):
             @pl.when(from_left >= 0)
             def _():
                 to_right(from_left, c).wait_recv()
@@ -177,20 +177,17 @@
             device_id_type=MESH,
         )
 
-    def other_core(i, carry):
-        core_send[i] = base_block(i * 2 + 1 - core).astype(BF16)
-        to_core(i).start()
-        return carry
-
-    lax.fori_loop(0, chips, other_core, 0)
-
-    def own_core(i, carry):
-        partial[i] = base_block(i * 2 + core)
-        return carry
-
-    lax.fori_loop(0, chips, own_core, 0)
-
-    forward(0)
+    passed = 0
+    for k in range(2 * chips):
+        i = k % chips
+        if k < chips:
+            core_send[i] = base_block(i * 2 + 1 - core).astype(BF16)
+            to_core(i).start()
+        else:
+            partial[i] = base_block(i * 2 + core)
+        upto = pieces * (k + 1) // (2 * chips)
+        forward(0, passed, upto)
+        passed = upto
 
     def to_chip(i, slot):
         return pltpu.make_async_remote_copy(
@@ -234,7 +231,7 @@
                 picked[...] += low_block(block)
 
     def step(s, carry):
-        forward(s + 1)
+        forward(s + 1, 0, pieces)
         low_of(s)
         return carry
 
@@ -326,9 +323,9 @@
     adp_dev, rank, kv = adapter_up.shape
     lanes = adp_dev * rank
     chips = n_hid // 2
-    pieces = 4 if n_tok <= 8 else 1
+    pieces = 8 if n_tok <= 8 else 1
     vmem = pl.BlockSpec(memory_space=pltpu.VMEM)
-    hbm = pl.BlockSpec(memory_space=pl.ANY)
+    hbm = pl.BlockSpec(memory_space=pltpu.HBM)
     dma = pltpu.SemaphoreType.DMA
     return pl.pallas_call(
         functools.partial(kernel, n_tok, n_hid, pieces, rank),

time: 39.4 us -> 39.1 us (level)
  Pallas kernels: 37.5 us -> 37.1 us
where the time goes in v2:
time: 39.1 us; the launch traced here: 38.9 us
  Pallas kernels  37.1 us (95%)
  local copies, waits for them, and re-layouts  1.77 us (5%)
    pallas_call x1, Pallas kernels, per_device(): pl.pallas_call(functools.partial(kernel, n_tok, n_hid, pieces, rank), out...  37.1 us
    unnamed x1, local copies, waits for them, and re-layouts  1.77 us

profile of v2, /device:TPU:0, one launch (start us, length us, event | category | flops | bytes accessed | tf_op | source)
XLA Modules:
  0.0 38.9 jit_solution(15800584861457107756)
XLA Ops:
  0.0 37.1 %shard_map.55 = bf16[768,256]{1,0:T(8,128)(2,1)} custom-call(s32[1,768]{1,0:T(1,128)} %bitcast.5, bf16[768,2048]{1,0:T(8,128)(2,1)} %tokens_hbm.1, bf16[2048,1024]{1,0:T(8,128)(2,1)} %value_hbm.1, bf16[128,2048]{1,0:T(8,128)(2,1)} %bitcast.3, bf16[128,256]{1,0:T(8,128)(2,1)} %bitcast.4), custom_call_target="tpu_custom_call" | custom-call | tf_op jit(solution)/shard_map/pallas_call | solution.py:330
  37.1 1.8 %copy.7 = bf16[768,256]{1,0:T(8,128)(2,1)} copy(bf16[768,256]{1,0:T(8,128)(2,1)} %shard_map.55) | data formatting | bytes 786432

commit v3 on v2

--- a/solution.py
+++ b/solution.py
@@ -16,6 +16,7 @@
     n_tok,
     n_hid,
     pieces,
+    extra,
     rank,
     ids_ref,
     tokens_hbm,
@@ -67,8 +68,6 @@
     load_value = pltpu.make_async_copy(value_hbm, value, load_sem.at[3])
     load_down.start()
     load_up.start()
-    load_tokens.start()
-    load_value.start()
 
     barrier = pltpu.get_barrier_semaphore()
     pl.semaphore_signal(barrier, inc=1, device_id={"parts": 1 - y}, device_id_type=MESH)
@@ -85,6 +84,11 @@
     def _():
         pl.semaphore_signal(barrier, inc=1, device_id={"tok": z + 1}, device_id_type=MESH)
 
+    load_down.wait()
+    load_up.wait()
+    load_tokens.start()
+    load_value.start()
+
     neighbours = (z > 0).astype(jnp.int32) + (z < n_tok - 1).astype(jnp.int32)
     pl.semaphore_wait(barrier, n_hid + neighbours)
 
@@ -92,8 +96,11 @@
         start = pl.multiple_of(side * half + c * piece, piece)
         return adapters.at[block, pl.ds(start, piece)]
 
+    def line_chunk(block, c):
+        return chunk(block, y, c) if c < pieces else chunk(block, 1 - y, c - extra)
+
     def to_right(block, c):
-        ref = chunk(block, y, c)
+        ref = line_chunk(block, c)
         return pltpu.make_async_remote_copy(
             src_ref=ref,
             dst_ref=ref,
@@ -104,7 +111,7 @@
         )
 
     def to_left(block, c):
-        ref = chunk(block, y, c)
+        ref = line_chunk(block, c)
         return pltpu.make_async_remote_copy(
             src_ref=ref,
             dst_ref=ref,
@@ -125,8 +132,6 @@
             device_id_type=MESH,
         )
 
-    load_down.wait()
-    load_up.wait()
     for c in range(pieces):
         @pl.when(z < n_tok - 1)
         def _():
@@ -136,11 +141,23 @@
         def _():
             to_left(z, c).start()
 
+    for c in range(pieces, pieces + extra):
+        @pl.when(z == 0)
+        def _():
+            to_right(z, c).start()
+
+        @pl.when(z == n_tok - 1)
+        def _():
+            to_left(z, c).start()
+
+    def by_pair(block, c):
+        return c < pieces - extra or (block != 0) & (block != n_tok - 1)
+
     def forward(s, first, last):
         from_left = z - 1 - s
         from_right = z + 1 + s
         for c in range(first, last):
-            @pl.when(from_left >= 0)
+            @pl.when(from_left >= 0 if c < pieces else from_left == 0)
             def _():
                 to_right(from_left, c).wait_recv()
 
@@ -148,9 +165,12 @@
                 def _():
                     to_right(from_left, c).start()
 
-                to_pair(from_left, y, c).start()
-
-            @pl.when(from_right < n_tok)
+                if c < pieces:
+                    @pl.when(by_pair(from_left, c))
+                    def _():
+                        to_pair(from_left, y, c).start()
+
+            @pl.when(from_right < n_tok if c < pieces else from_right == n_tok - 1)
             def _():
                 to_left(from_right, c).wait_recv()
 
@@ -158,7 +178,10 @@
                 def _():
                     to_left(from_right, c).start()
 
-                to_pair(from_right, y, c).start()
+                if c < pieces:
+                    @pl.when(by_pair(from_right, c))
+                    def _():
+                        to_pair(from_right, y, c).start()
 
     load_tokens.wait()
     load_value.wait()
@@ -189,6 +212,8 @@
         forward(0, passed, upto)
         passed = upto
 
+    forward(0, pieces, pieces + extra)
+
     def to_chip(i, slot):
         return pltpu.make_async_remote_copy(
             src_ref=chip_send.at[i],
@@ -227,11 +252,14 @@
             @pl.when((block >= 0) & (block < n_tok))
             def _():
                 for c in range(pieces):
-                    to_pair(block, 1 - y, c).wait_recv()
+                    @pl.when(by_pair(block, c))
+                    def _():
+                        to_pair(block, 1 - y, c).wait_recv()
+
                 picked[...] += low_block(block)
 
     def step(s, carry):
-        forward(s + 1, 0, pieces)
+        forward(s + 1, 0, pieces + extra)
         low_of(s)
         return carry
 
@@ -300,18 +328,19 @@
         to_chip(lax.rem(x + d, chips), x).wait_send()
 
     def drain(block, carry):
-        for c in range(pieces):
-            @pl.when((block <= z) & (z < n_tok - 1))
+        for c in range(pieces + extra):
+            @pl.when((block <= z if c < pieces else block == 0) & (z < n_tok - 1))
             def _():
                 to_right(block, c).wait_send()
 
-            @pl.when((block >= z) & (z > 0))
+            @pl.when((block >= z if c < pieces else block == n_tok - 1) & (z > 0))
             def _():
                 to_left(block, c).wait_send()
 
-            @pl.when(block != z)
-            def _():
-                to_pair(block, y, c).wait_send()
+            if c < pieces:
+                @pl.when((block != z) & by_pair(block, c))
+                def _():
+                    to_pair(block, y, c).wait_send()
 
         return carry
 
@@ -324,11 +353,12 @@
     lanes = adp_dev * rank
     chips = n_hid // 2
     pieces = 8 if n_tok <= 8 else 1
+    extra = 2 if pieces == 8 else 0
     vmem = pl.BlockSpec(memory_space=pltpu.VMEM)
     hbm = pl.BlockSpec(memory_space=pltpu.HBM)
     dma = pltpu.SemaphoreType.DMA
     return pl.pallas_call(
-        functools.partial(kernel, n_tok, n_hid, pieces, rank),
+        functools.partial(kernel, n_tok, n_hid, pieces, extra, rank),
         out_shape=jax.ShapeDtypeStruct((rows, kv), BF16),
         in_specs=[vmem, hbm, hbm, hbm, hbm],
         out_specs=vmem,
@@ -346,9 +376,9 @@
             pltpu.VMEM((rank, rows), BF16),
             pltpu.VMEM((n_hid, rank, rows), BF16),
             dma((4,)),
-            dma((n_tok, pieces)),
-            dma((n_tok, pieces)),
-            dma((n_tok, pieces)),
+            dma((n_tok, pieces + extra)),
+            dma((n_tok, pieces + extra)),
+            dma((n_tok, pieces + extra)),
             dma((n_tok, pieces)),
             dma((n_tok, pieces)),
             dma((chips,)),

time: 39.1 us -> 38.5 us (0.985)
  Pallas kernels: 37.1 us -> 36.5 us
    pallas_call x1, Pallas kernels: 37.1 us -> 36.5 us  [per_device(): pl.pallas_call(functools.partial(kernel, n_tok, n_hid, pieces, extra, ran...]
where the time goes in v3:
time: 38.5 us; the launch traced here: 38.3 us
  Pallas kernels  36.5 us (95%)
  local copies, waits for them, and re-layouts  1.77 us (5%)
    pallas_call x1, Pallas kernels, per_device(): pl.pallas_call(functools.partial(kernel, n_tok, n_hid, pieces, extra, ran...  36.5 us
    unnamed x1, local copies, waits for them, and re-layouts  1.77 us

profile of v3, /device:TPU:0, one launch (start us, length us, event | category | flops | bytes accessed | tf_op | source)
XLA Modules:
  0.0 38.3 jit_solution(12441064921199597044)
XLA Ops:
  0.0 36.5 %shard_map.55 = bf16[768,256]{1,0:T(8,128)(2,1)} custom-call(s32[1,768]{1,0:T(1,128)} %bitcast.5, bf16[768,2048]{1,0:T(8,128)(2,1)} %tokens_hbm.1, bf16[2048,1024]{1,0:T(8,128)(2,1)} %value_hbm.1, bf16[128,2048]{1,0:T(8,128)(2,1)} %bitcast.3, bf16[128,256]{1,0:T(8,128)(2,1)} %bitcast.4), custom_call_target="tpu_custom_call" | custom-call | tf_op jit(solution)/shard_map/pallas_call | solution.py:360
  36.5 1.8 %copy.7 = bf16[768,256]{1,0:T(8,128)(2,1)} copy(bf16[768,256]{1,0:T(8,128)(2,1)} %shard_map.55) | data formatting | bytes 786432
